TPU v7x, 32 devices: a whole 2x2x4 slice. The times are simulated.
32 devices in a mesh: lat: 8 (over z, x), lev: 4 (over y, core).
Axes of the slice: x: 2, y: 2, z: 4, core: 2. Of those that a mesh axis runs over, the one named last changes fastest.
Arguments:
- fourier: bfloat16 [1280, 640, 1024], P('lat', None, 'lev'), may hold values from -6 to 6
- legendre: bfloat16 [640, 2, 640, 320], P('lat', None, 'lev'), may hold values from -0.25 to 0.25
- owner: int32 [640], replicated, may hold values from 0 to 7, as said below
Outputs:
- spectral: bfloat16 [640, 2, 320, 1024], P('lat', None, None, 'lev')
Inputs may be any that keep to these rules, and one draw needn't show every extreme that they name: `owner`: each index along lat is named by exactly 80 wavenumbers.
All inputs are finite; a program needn't handle non-finite values.
Results may differ from a plain program's by a relative error of at most 0.0051.
Values may be sent and summed in bfloat16 or wider, within the bound.
A program may use at most 384 MiB of HBM per device.

v0:
```python
import functools

import jax
import jax.numpy as jnp
from jax import lax
from jax.experimental import pallas as pl
from jax.experimental.pallas import tpu as pltpu
from jax.sharding import PartitionSpec as P

CHUNKS = 2


def slot_places(owner, slot_count):
    wave_count = owner.shape[0]
    wave_ids = jnp.arange(wave_count, dtype=jnp.int32)
    earlier = (owner[None, :] == owner[:, None]) & (wave_ids[None, :] < wave_ids[:, None])
    ranked = jnp.sum(earlier.astype(jnp.int32), axis=1)
    placed = owner * slot_count + ranked
    return placed[None, :] == wave_ids[:, None]


def project(base, wave_count, waves_ref, rows_ref, table_ref, *rest):
    out_ref = rest[-1]
    half_rows, column_count = out_ref.shape[2:]
    half = rows_ref.shape[0] // 2
    upper = rows_ref[:half, 0].astype(jnp.float32).reshape(-1, column_count)
    lower = rows_ref[half:, 0].astype(jnp.float32).reshape(-1, column_count)
    wave = waves_ref[base + pl.program_id(0)]
    degree = lax.broadcasted_iota(jnp.int32, (half_rows, column_count), 0)
    for parity in range(2):
        part = (upper + lower if parity == 0 else upper - lower).astype(jnp.bfloat16)
        total = lax.dot_general(
            table_ref[0, parity], part, (((0,), (0,)), ((), ())),
            preferred_element_type=jnp.float32,
        )
        live = (wave_count - wave - parity + 1) // 2
        out_ref[0, parity] = jnp.where(degree < live, total, 0.0).astype(out_ref.dtype)


def project_chunk(base, wave_count, own_waves, rows, table, previous):
    groups, chunk_slots, group_rows, column_count = rows.shape
    slot_count, _, north_count, half_rows = table.shape
    in_specs = [
        pl.BlockSpec((groups, 1, group_rows, column_count), lambda s, w: (0, s, 0, 0)),
        pl.BlockSpec((1, 2, north_count, half_rows), lambda s, w: (base + s, 0, 0, 0)),
    ]
    operands = [own_waves, rows, table]
    aliases = {}
    if previous is not None:
        in_specs.append(pl.BlockSpec(memory_space=pl.ANY))
        operands.append(previous)
        aliases = {3: 0}
    return pl.pallas_call(
        functools.partial(project, base, wave_count),
        grid_spec=pltpu.PrefetchScalarGridSpec(
            num_scalar_prefetch=1,
            grid=(chunk_slots,),
            in_specs=in_specs,
            out_specs=pl.BlockSpec(
                (1, 2, half_rows, column_count), lambda s, w: (base + s, 0, 0, 0)
            ),
        ),
        out_shape=jax.ShapeDtypeStruct(
            (slot_count, 2, half_rows, column_count), jnp.bfloat16
        ),
        input_output_aliases=aliases,
        compiler_params=pltpu.CompilerParams(vmem_limit_bytes=32 * 1024 * 1024),
        cost_estimate=pl.CostEstimate(
            flops=4 * chunk_slots * north_count * half_rows * column_count,
            bytes_accessed=2 * rows.size
            + 4 * chunk_slots * half_rows * (north_count + column_count),
            transcendentals=0,
        ),
    )(*operands)


def body(fourier, legendre, owner):
    lat_count = lax.axis_size("lat")
    row_count, wave_count, column_count = fourier.shape
    slot_count = wave_count // lat_count
    matched = slot_places(owner, slot_count)
    wave_ids = jnp.arange(wave_count, dtype=jnp.int32)
    wave_of = jnp.sum(jnp.where(matched, wave_ids[None, :], 0), axis=1)
    own_waves = lax.dynamic_slice_in_dim(wave_of, lax.axis_index("lat") * slot_count, slot_count)
    table = lax.all_gather(legendre, "lev", axis=2, tiled=True)
    picks = matched.astype(jnp.bfloat16).reshape(lat_count, slot_count, wave_count)
    chunks = CHUNKS if slot_count % CHUNKS == 0 else 1
    chunk_slots = slot_count // chunks
    result = None
    for chunk in range(chunks):
        base = chunk * chunk_slots
        pick = picks[:, base : base + chunk_slots].reshape(-1, wave_count)
        outgoing = lax.dot_general(
            pick, fourier, (((1,), (1,)), ((), ())), preferred_element_type=jnp.bfloat16
        )
        arrived = lax.all_to_all(outgoing, "lat", split_axis=0, concat_axis=0, tiled=True)
        arrived = arrived.reshape(lat_count, chunk_slots, row_count, column_count)
        if row_count % 16 != 0:
            arrived = arrived.reshape(2, lat_count // 2, chunk_slots, row_count, column_count)
            arrived = arrived.swapaxes(1, 2).reshape(2, chunk_slots, -1, column_count)
        result = project_chunk(base, wave_count, own_waves, arrived, table, result)
    return result


def solution(mesh):
    placed = (P("lat", None, "lev"), P("lat", None, "lev", None), P())
    return jax.shard_map(
        body, mesh=mesh, in_specs=placed, out_specs=P("lat", None, None, "lev"), check_vma=False
    )
```

profile of v0, /device:TPU:0, one launch (start us, length us, event | category | flops | bytes accessed | tf_op | source)
XLA Modules:
  0.0 1291.4 jit_solution(289883555846234481)
XLA Ops:
  6.5 0.0 all-gather.2.cloned.1.call-start
  6.5 0.7 all-gather.2.cloned.1.call-update
  7.3 1.1 convert_reduce_fusion
  8.3 0.7 multiply_add_fusion.1
  9.0 0.3 broadcast_compare_fusion
  9.3 0.1 fusion.1
  9.4 50.7 %fusion.3 = bf16[320,160,256]{2,0,1:T(8,128)(2,1)} fusion(pred[320,640,1]{1,0,2:T(8,128)(4,1)S(1)} %bitcast.13, bf16[160,640,256]{2,1,0:T(8,128)(2,1)} %param.3), kind=kOutput, calls=%fused_computation.10 | convolution fusion | flops 16777216000 | bytes 78848000 | tf_op jit(solution)/shard_map/dot_general | solution.py:93
  60.0 34.2 %copy.10 = bf16[320,160,256]{2,1,0:T(8,128)(2,1)} copy(bf16[320,160,256]{2,0,1:T(8,128)(2,1)} %fusion.3) | data formatting | bytes 52428800 | tf_op jit(solution)/shard_map/dot_general | solution.py:93
  94.2 7.2 all-to-all-start.1
  101.5 40.8 %fusion.2 = bf16[320,160,256]{2,0,1:T(8,128)(2,1)} fusion(pred[320,640,1]{1,0,2:T(8,128)(4,1)S(1)} %bitcast.12, bf16[160,640,256]{2,1,0:T(8,128)(2,1)} %param.3), kind=kOutput, calls=%fused_computation.9 | convolution fusion | flops 16777216000 | bytes 78848000 | tf_op jit(solution)/shard_map/dot_general | solution.py:93
  142.3 34.0 %copy.9 = bf16[320,160,256]{2,1,0:T(8,128)(2,1)} copy(bf16[320,160,256]{2,0,1:T(8,128)(2,1)} %fusion.2) | data formatting | bytes 52428800 | tf_op jit(solution)/shard_map/dot_general | solution.py:93
  176.2 492.0 %all-to-all-done.1 = bf16[320,160,256]{2,1,0:T(8,128)(2,1)} async-done(((bf16[320,160,256]{2,1,0:T(8,128)(2,1)}), bf16[320,160,256]{2,1,0:T(8,128)(2,1)}, u32[]{:S(2)}, u32[]{:S(2)}) %all-to-all-start.1) | async-done | bytes 26214432 | tf_op jit(solution)/shard_map/all_to_all | solution.py:96
  668.2 6.7 all-to-all-start
  674.9 0.2 select_reduce_fusion
  675.1 0.1 dynamic_slice.3.waves_ref
  675.2 0.0 all-gather.2.cloned.1.call-done.table_ref
  675.2 44.9 %shard_map.37.rest_0_ = bf16[80,2,320,256]{3,2,1,0:T(8,128)(2,1)} custom-call(s32[80]{0:T(128)S(1)} %dynamic_slice.3.waves_ref, bf16[8,40,160,256]{3,2,1,0:T(8,128)(2,1)} %bitcast.5.rows_ref, bf16[80,2,640,320]{3,2,1,0:T(8,128)(2,1)} %all-gather.2.cloned.1.call-done.table_ref), custom_call_target="tpu_custom_call" | custom-call | flops 8388608000 | bytes 72089600 | tf_op jit(solution)/shard_map/pallas_call | solution.py:53
  720.1 519.5 %all-to-all-done = bf16[320,160,256]{2,1,0:T(8,128)(2,1)} async-done(((bf16[320,160,256]{2,1,0:T(8,128)(2,1)}), bf16[320,160,256]{2,1,0:T(8,128)(2,1)}, u32[]{:S(2)}, u32[]{:S(2)}) %all-to-all-start) | async-done | bytes 26214432 | tf_op jit(solution)/shard_map/all_to_all | solution.py:96
  1239.6 45.0 %shard_map.38 = bf16[80,2,320,256]{3,2,1,0:T(8,128)(2,1)} custom-call(s32[80]{0:T(128)S(1)} %dynamic_slice.3.waves_ref, bf16[8,40,160,256]{3,2,1,0:T(8,128)(2,1)} %bitcast.2.rows_ref, bf16[80,2,640,320]{3,2,1,0:T(8,128)(2,1)} %all-gather.2.cloned.1.call-done.table_ref, bf16[80,2,320,256]{3,2,1,0:T(8,128)(2,1)} %shard_map.37.rest_0_), custom_call_target="tpu_custom_call", output_to_operand_aliasing={{}: (3, {})} | custom-call | flops 8388608000 | bytes 72089600 | tf_op jit(solution)/shard_map/pallas_call | solution.py:53
  (1 shorter events, 0.0 us)
Async XLA Ops:
  6.5 668.7 %all-gather.2.cloned.1.call-start = ((), (), s32[]{:S(2)}) async-start(), calls=%async_computation.2 | async-start | bytes 98304000 | tf_op jit(solution)/shard_map/all_gather | solution.py:85
  94.2 574.0 %all-to-all-start.1 = ((bf16[320,160,256]{2,1,0:T(8,128)(2,1)}), bf16[320,160,256]{2,1,0:T(8,128)(2,1)}, u32[]{:S(2)}, u32[]{:S(2)}) async-start(bf16[320,160,256]{2,1,0:T(8,128)(2,1)} %copy.10), calls=%async_computation.1 | async-start | bytes 52428800 | tf_op jit(solution)/shard_map/all_to_all | solution.py:96
  668.2 571.4 %all-to-all-start = ((bf16[320,160,256]{2,1,0:T(8,128)(2,1)}), bf16[320,160,256]{2,1,0:T(8,128)(2,1)}, u32[]{:S(2)}, u32[]{:S(2)}) async-start(bf16[320,160,256]{2,1,0:T(8,128)(2,1)} %copy.9), calls=%async_computation | async-start | bytes 52428800 | tf_op jit(solution)/shard_map/all_to_all | solution.py:96
Sparse Core Ops, SparseCore 0:
  8.9 461.6 all-gather.1
where the time goes:
time: 1290 us
  waiting for transfers between devices  1010 us (78%)
  matrix products  91.5 us (7%)
  Pallas kernels  89.9 us (7%)
  local copies, waits for them, and re-layouts  68.3 us (5%)
  starting transfers between devices  13.9 us (1%)
  between operations  13.4 us (1%)
    all_to_all x2, waiting for transfers between devices, body(): lax.all_to_all(outgoing, 'lat', split_axis=0, concat_axis=0, tiled=True)  1010 us
    dot_general x2, matrix products, body(): lax.dot_general(pick, fourier, (((1,), (1,)), ((), ())), preferred_elemen...  91.5 us
    pallas_call x2, Pallas kernels, project_chunk(): pl.pallas_call(functools.partial(project, base, wave_count), grid_spec=pl...  89.9 us
    dot_general x2, local copies, waits for them, and re-layouts, body(): lax.dot_general(pick, fourier, (((1,), (1,)), ((), ())), preferred_elemen...  68.1 us
  transfers between devices with their start and end apart: 3, of which 2 were waited for; matrix products, arithmetic and copies ran while one was open for 13% of the time, Pallas kernels for 3%

commit v1 on v0

--- a/solution.py
+++ b/solution.py
@@ -8,6 +8,307 @@
 from jax.sharding import PartitionSpec as P
 
 CHUNKS = 2
+GROUP = 8
+PIECE = 2
+ROWS = 16
+
+
+def ranks(owner, slot_count):
+    wave_count = owner.shape[0]
+    wave_ids = jnp.arange(wave_count, dtype=jnp.int32)
+    earlier = (owner[None, :] == owner[:, None]) & (wave_ids[None, :] < wave_ids[:, None])
+    ranked = jnp.sum(earlier.astype(jnp.int32), axis=1)
+    return owner * slot_count + ranked
+
+
+def flipped(index, mask):
+    bit = 1
+    result = index
+    while bit <= mask:
+        if mask & bit:
+            result = result + bit * (1 - 2 * lax.rem(lax.div(index, bit), 2))
+        bit *= 2
+    return result
+
+
+def far_first(count):
+    half = count // 2
+    far = [half + m for m in range(half)]
+    near = [m for m in range(1, half)]
+    order = sorted(far, key=lambda m: (m & 1, -m)) + sorted(near, key=lambda m: (m == 1, m))
+    return order
+
+
+def exchange(
+    fourier_ref, picks_ref, table_ref,
+    out_ref, send_ref, land_ref, tables_ref,
+    block, drawn, packed, rows, table, made, even, odd,
+    block_sem, packed_sem, send_first, recv_first, send_sem, recv_sem,
+    table_send, table_recv, load_sem, store_sem,
+):
+    lat_count, slot_count, row_count, column_count = send_ref.shape
+    half_rows = table_ref.shape[3]
+    lev_count = tables_ref.shape[0] + 1
+    chunks = slot_count // GROUP
+    blocks = row_count // ROWS
+    pieces = GROUP // PIECE
+    me, lev = lax.axis_index("lat"), lax.axis_index("lev")
+    order = far_first(lat_count)
+    peers = {m: (flipped(me, m), lev) for m in order}
+    sides = {m: (me, flipped(lev, m)) for m in range(1, lev_count)}
+    mesh_ids = pl.DeviceIdType.MESH
+
+    barrier = pltpu.get_barrier_semaphore()
+    for peer in [*peers.values(), *sides.values()]:
+        pl.semaphore_signal(barrier, inc=1, device_id=peer, device_id_type=mesh_ids)
+    pl.semaphore_wait(barrier, len(peers) + len(sides))
+
+    def table_copy(chunk, mask):
+        span = pl.ds(chunk * GROUP, GROUP)
+        return pltpu.make_async_remote_copy(
+            src_ref=table_ref.at[span], dst_ref=tables_ref.at[mask - 1, span],
+            send_sem=table_send.at[chunk, mask - 1], recv_sem=table_recv.at[chunk, mask - 1],
+            device_id=sides[mask], device_id_type=mesh_ids,
+        )
+
+    def first_copy(step, mask):
+        span = (pl.ds(0, GROUP), pl.ds(step * ROWS, ROWS))
+        return pltpu.make_async_remote_copy(
+            src_ref=send_ref.at[(mask, *span)], dst_ref=land_ref.at[(mask - 1, *span)],
+            send_sem=send_first.at[step, mask - 1], recv_sem=recv_first.at[step, mask - 1],
+            device_id=peers[mask], device_id_type=mesh_ids,
+        )
+
+    def later_copy(piece, mask):
+        span = pl.ds(piece * PIECE, PIECE)
+        return pltpu.make_async_remote_copy(
+            src_ref=send_ref.at[mask, span], dst_ref=land_ref.at[mask - 1, span],
+            send_sem=send_sem.at[piece, mask - 1], recv_sem=recv_sem.at[piece, mask - 1],
+            device_id=peers[mask], device_id_type=mesh_ids,
+        )
+
+    def block_copy(step, side):
+        return pltpu.make_async_copy(
+            fourier_ref.at[pl.ds(step * ROWS, ROWS)], block.at[side], block_sem.at[side]
+        )
+
+    def pick(chunk, after):
+        block_copy(0, 0).start()
+
+        def one(step, carry):
+            side = lax.rem(step, 2)
+
+            @pl.when(step + 1 < blocks)
+            def _():
+                block_copy(step + 1, 1 - side).start()
+
+            block_copy(step, side).wait()
+
+            def row(r, inner):
+                drawn[:, r, :] = jnp.dot(
+                    picks_ref[chunk], block[side, r], preferred_element_type=jnp.float32
+                )
+                return inner
+
+            for r in range(ROWS):
+                row(r, 0)
+            packed[...] = drawn[...].astype(packed.dtype).reshape(packed.shape)
+            copy = pltpu.make_async_copy(
+                packed,
+                send_ref.at[:, pl.ds(chunk * GROUP, GROUP), pl.ds(step * ROWS, ROWS)],
+                packed_sem,
+            )
+            copy.start()
+            copy.wait()
+            after(step)
+            return carry
+
+        lax.fori_loop(0, blocks, one, 0)
+
+    def project(piece):
+        span = pl.ds(piece * PIECE, PIECE)
+        copies = [pltpu.make_async_copy(send_ref.at[0, span], rows.at[:, me], load_sem.at[0])]
+        for m in order:
+            copies.append(pltpu.make_async_copy(
+                land_ref.at[m - 1, span], rows.at[:, peers[m][0]], load_sem.at[m]))
+        for m in range(lev_count):
+            source = table_ref.at[span] if m == 0 else tables_ref.at[m - 1, span]
+            start = pl.multiple_of((lev if m == 0 else sides[m][1]) * row_count, ROWS)
+            copies.append(pltpu.make_async_copy(
+                source, table.at[:, :, pl.ds(start, row_count)], load_sem.at[lat_count + m]))
+        for copy in copies:
+            copy.start()
+        for copy in copies:
+            copy.wait()
+
+        def one(i, carry):
+            half = lat_count // 2
+            upper = rows[i, :half].astype(jnp.float32).reshape(-1, column_count)
+            lower = rows[i, half:].astype(jnp.float32).reshape(-1, column_count)
+            even[...] = (upper + lower).astype(even.dtype)
+            odd[...] = (upper - lower).astype(odd.dtype)
+            for parity, part in enumerate((even, odd)):
+                total = lax.dot_general(
+                    table[i, parity], part[...], (((0,), (0,)), ((), ())),
+                    preferred_element_type=jnp.float32,
+                )
+                made[i, parity] = total.astype(made.dtype)
+            return carry
+
+        lax.fori_loop(0, PIECE, one, 0)
+        copy = pltpu.make_async_copy(made, out_ref.at[span], store_sem)
+        copy.start()
+        copy.wait()
+
+    def start_tables(chunk):
+        for m in sides:
+            table_copy(chunk, m).start()
+
+    def send_rows(step):
+        for m in order:
+            first_copy(step, m).start()
+
+    def send_chunk(chunk):
+        def one(p, carry):
+            for m in order:
+                later_copy(chunk * pieces + p, m).start()
+            return carry
+
+        lax.fori_loop(0, pieces, one, 0)
+
+    def project_chunk(chunk):
+        def one(p, carry):
+            for m in order:
+                later_copy(chunk * pieces + p, m).wait_recv()
+            project(chunk * pieces + p)
+            return carry
+
+        for m in sides:
+            table_copy(chunk, m).wait_recv()
+        lax.fori_loop(0, pieces, one, 0)
+
+    def first_chunk():
+        def landed(step, carry):
+            for m in order:
+                first_copy(step, m).wait_recv()
+            return carry
+
+        def one(p, carry):
+            project(p)
+            return carry
+
+        for m in sides:
+            table_copy(0, m).wait_recv()
+        lax.fori_loop(0, blocks, landed, 0)
+        lax.fori_loop(0, pieces, one, 0)
+
+    def nothing(step):
+        del step
+
+    pick_start = 1
+    pick(0, send_rows)
+    start_tables(0)
+    pick(pick_start, nothing)
+    start_tables(1)
+    send_chunk(1)
+
+    def stage(chunk, carry):
+        pick(chunk, nothing)
+        start_tables(chunk)
+        send_chunk(chunk)
+
+        @pl.when(chunk == 2)
+        def _():
+            first_chunk()
+
+        @pl.when(chunk > 2)
+        def _():
+            project_chunk(chunk - 2)
+
+        return carry
+
+    lax.fori_loop(2, chunks, stage, 0)
+    project_chunk(chunks - 2)
+    project_chunk(chunks - 1)
+
+    def drain_first(step, carry):
+        for m in order:
+            first_copy(step, m).wait_send()
+        return carry
+
+    def drain_later(piece, carry):
+        for m in order:
+            later_copy(piece, m).wait_send()
+        return carry
+
+    def drain_tables(chunk, carry):
+        for m in sides:
+            table_copy(chunk, m).wait_send()
+        return carry
+
+    lax.fori_loop(0, blocks, drain_first, 0)
+    lax.fori_loop(pieces, chunks * pieces, drain_later, 0)
+    lax.fori_loop(0, chunks, drain_tables, 0)
+
+
+def direct_body(fourier, legendre, owner):
+    lat_count, lev_count = lax.axis_size("lat"), lax.axis_size("lev")
+    row_count, wave_count, column_count = fourier.shape
+    half_rows = legendre.shape[3]
+    slot_count = wave_count // lat_count
+    chunks, blocks, pieces = slot_count // GROUP, row_count // ROWS, slot_count // PIECE
+    me = lax.axis_index("lat")
+    placed = ranks(owner, slot_count)
+    shape = (chunks, lat_count, GROUP)
+    slot_ids = (
+        (me ^ lax.broadcasted_iota(jnp.int32, shape, 1)) * slot_count
+        + lax.broadcasted_iota(jnp.int32, shape, 0) * GROUP
+        + lax.broadcasted_iota(jnp.int32, shape, 2)
+    ).reshape(chunks, lat_count * GROUP)
+    picks = (placed[None, None, :] == slot_ids[:, :, None]).astype(jnp.bfloat16)
+    own = me * slot_count + jnp.arange(slot_count, dtype=jnp.int32)
+    wave_ids = jnp.arange(wave_count, dtype=jnp.int32)
+    waves = jnp.sum(jnp.where(placed[None, :] == own[:, None], wave_ids[None, :], 0), axis=1)
+    dtype = jnp.bfloat16
+    anywhere = pl.BlockSpec(memory_space=pl.ANY)
+    made, *_ = pl.pallas_call(
+        exchange,
+        in_specs=[anywhere, pl.BlockSpec(memory_space=pltpu.VMEM), anywhere],
+        out_specs=[anywhere] * 4,
+        out_shape=[
+            jax.ShapeDtypeStruct((slot_count, 2, half_rows, column_count), dtype),
+            jax.ShapeDtypeStruct((lat_count, slot_count, row_count, column_count), dtype),
+            jax.ShapeDtypeStruct((lat_count - 1, slot_count, row_count, column_count), dtype),
+            jax.ShapeDtypeStruct((lev_count - 1, *legendre.shape), dtype),
+        ],
+        scratch_shapes=[
+            pltpu.VMEM((2, ROWS, wave_count, column_count), dtype),
+            pltpu.VMEM((lat_count * GROUP, ROWS, column_count), jnp.float32),
+            pltpu.VMEM((lat_count, GROUP, ROWS, column_count), dtype),
+            pltpu.VMEM((PIECE, lat_count, row_count, column_count), dtype),
+            pltpu.VMEM((PIECE, 2, lev_count * row_count, half_rows), dtype),
+            pltpu.VMEM((PIECE, 2, half_rows, column_count), dtype),
+            pltpu.VMEM((lat_count // 2 * row_count, column_count), dtype),
+            pltpu.VMEM((lat_count // 2 * row_count, column_count), dtype),
+            pltpu.SemaphoreType.DMA((2,)),
+            pltpu.SemaphoreType.DMA,
+            pltpu.SemaphoreType.DMA((blocks, lat_count - 1)),
+            pltpu.SemaphoreType.DMA((blocks, lat_count - 1)),
+            pltpu.SemaphoreType.DMA((pieces, lat_count - 1)),
+            pltpu.SemaphoreType.DMA((pieces, lat_count - 1)),
+            pltpu.SemaphoreType.DMA((chunks, lev_count - 1)),
+            pltpu.SemaphoreType.DMA((chunks, lev_count - 1)),
+            pltpu.SemaphoreType.DMA((lat_count + lev_count,)),
+            pltpu.SemaphoreType.DMA,
+        ],
+        compiler_params=pltpu.CompilerParams(
+            collective_id=0, has_side_effects=True, vmem_limit_bytes=48 * 1024 * 1024
+        ),
+    )(fourier, picks, legendre)
+    parity = jnp.arange(2, dtype=jnp.int32)
+    live = (wave_count - waves[:, None] - parity[None, :] + 1) // 2
+    degree = lax.broadcasted_iota(jnp.int32, made.shape, 2)
+    return jnp.where(degree < live[:, :, None, None], made, jnp.zeros_like(made))
 
 
 def slot_places(owner, slot_count):
@@ -102,8 +403,33 @@
     return result
 
 
+def direct_fits(mesh):
+    counts = (mesh.shape["lat"], mesh.shape["lev"])
+    return all(n & (n - 1) == 0 and 2 <= n <= 8 for n in counts) and counts[0] >= 4
+
+
+def routed(mesh):
+    lat_count, lev_count = mesh.shape["lat"], mesh.shape["lev"]
+
+    def body_of(fourier, legendre, owner):
+        row_count, wave_count, _ = fourier.shape
+        slot_count = wave_count // lat_count
+        fits = (
+            direct_fits(mesh)
+            and row_count % ROWS == 0
+            and slot_count % GROUP == 0
+            and slot_count // GROUP >= 4
+            and row_count * lat_count // 2 == legendre.shape[2] * lev_count
+            and legendre.shape[2] == row_count
+        )
+        return (direct_body if fits else body)(fourier, legendre, owner)
+
+    return body_of
+
+
 def solution(mesh):
     placed = (P("lat", None, "lev"), P("lat", None, "lev", None), P())
     return jax.shard_map(
-        body, mesh=mesh, in_specs=placed, out_specs=P("lat", None, None, "lev"), check_vma=False
+        routed(mesh), mesh=mesh, in_specs=placed, out_specs=P("lat", None, None, "lev"),
+        check_vma=False,
     )

time: 1290 us -> 1180 us (0.915)
  Pallas kernels: 89.9 us -> 1150 us
  waiting for transfers between devices: 1010 us -> 0 us
  matrix products: 91.5 us -> 0 us
  local copies, waits for them, and re-layouts: 68.3 us -> 0.24 us
  other arithmetic: 2.3 us -> 27.4 us
  starting transfers between devices: 13.9 us -> 0 us
  between operations: 13.4 us -> 0.05 us
    pallas_call x2 -> x1, Pallas kernels: 89.9 us -> 1150 us  [direct_body(): pl.pallas_call(exchange, in_specs=[anywhere, pl.BlockSpec(memory_space=pl...]
    all_to_all x2 -> x0, waiting for transfers between devices: 1010 us -> none  [body(): lax.all_to_all(outgoing, 'lat', split_axis=0, concat_axis=0, tiled=True)]
    dot_general x2 -> x0, matrix products: 91.5 us -> none  [body(): lax.dot_general(pick, fourier, (((1,), (1,)), ((), ())), preferred_elemen...]
    dot_general x2 -> x0, local copies, waits for them, and re-layouts: 68.1 us -> none  [body(): lax.dot_general(pick, fourier, (((1,), (1,)), ((), ())), preferred_elemen...]
    select_n x0 -> x2, other arithmetic: none -> 25.2 us  [the longest x1 25.1 us: direct_body(): jnp.where(degree < live[:, :, None, None], made, jnp.zeros_like(made))]
    all_to_all x2 -> x0, starting transfers between devices: 13.9 us -> none  [body(): lax.all_to_all(outgoing, 'lat', split_axis=0, concat_axis=0, tiled=True)]
  transfers between devices with their start and end apart: 3 -> 0, of which waited for: 2 -> 0; matrix products, arithmetic and copies ran while one was open for 13% -> 0% of each run, Pallas kernels for 3% -> 0%
where the time goes in v1:
time: 1180 us
  Pallas kernels  1150 us (97%)
  other arithmetic  27.4 us (2%)
    pallas_call x1, Pallas kernels, direct_body(): pl.pallas_call(exchange, in_specs=[anywhere, pl.BlockSpec(memory_space=pl...  1150 us
    select_n x1, other arithmetic, direct_body(): jnp.where(degree < live[:, :, None, None], made, jnp.zeros_like(made))  25.1 us

profile of v1, /device:TPU:0, one launch (start us, length us, event | category | flops | bytes accessed | tf_op | source)
XLA Modules:
  0.0 1177.8 jit_solution(8579205608315506889)
XLA Ops:
  0.0 0.1 iota.54
  0.1 0.1 mul.33
  0.2 0.1 iota.59
  0.2 0.1 add_add_fusion
  0.3 1.1 convert_reduce_fusion
  1.4 0.7 multiply_add_fusion
  2.1 0.2 compare_convert_fusion.picks_ref
  2.3 1150.0 %shard_map.37 = (bf16[80,2,320,256]{3,2,1,0:T(8,128)(2,1)}, bf16[8,80,160,256]{3,2,1,0:T(8,128)(2,1)}, bf16[7,80,160,256]{3,2,1,0:T(8,128)(2,1)}, bf16[3,80,2,160,320]{4,3,2,1,0:T(8,128)(2,1)}) custom-call(bf16[160,640,256]{2,1,0:T(8,128)(2,1)} %fourier_ref.1, bf16[10,64,640]{2,1,0:T(8,128)(2,1)S(1)} %compare_convert_fusion.picks_ref, ...), custom_call_target="tpu_custom_call" | custom-call | tf_op jit(solution)/shard_map/pallas_call | solution.py:274
  1152.4 0.2 select_reduce_fusion
  1152.6 0.1 add_select_fusion
  1152.7 25.1 %fusion = bf16[80,2,320,256]{3,2,1,0:T(8,128)(2,1)} fusion(bf16[80,2,320,256]{3,2,1,0:T(8,128)(2,1)} %get-tuple-element.6, s32[80,2]{1,0:T(8,128)S(1)} %add_select_fusion), kind=kLoop, calls=%fused_computation.1 | loop fusion | flops 26214400 | bytes 52429440 | tf_op jit(solution)/shard_map/jit(_where)/select_n | solution.py:311
  (5 shorter events, 0.0 us)

commit v2 on v1

--- a/solution.py
+++ b/solution.py
@@ -11,6 +11,7 @@
 GROUP = 8
 PIECE = 2
 ROWS = 16
+MADE_ELEMENTS = 8 * 1024 * 1024
 
 
 def ranks(owner, slot_count):
@@ -40,11 +41,12 @@
 
 
 def exchange(
-    fourier_ref, picks_ref, table_ref,
+    live_ref, fourier_ref, picks_ref, table_ref,
     out_ref, send_ref, land_ref, tables_ref,
-    block, drawn, packed, rows, table, made, even, odd,
+    block, drawn, packed, rows, table, even, odd,
     block_sem, packed_sem, send_first, recv_first, send_sem, recv_sem,
-    table_send, table_recv, load_sem, store_sem,
+    send_last, recv_last,
+    table_send, table_recv, load_sem,
 ):
     lat_count, slot_count, row_count, column_count = send_ref.shape
     half_rows = table_ref.shape[3]
@@ -61,6 +63,10 @@
     barrier = pltpu.get_barrier_semaphore()
     for peer in [*peers.values(), *sides.values()]:
         pl.semaphore_signal(barrier, inc=1, device_id=peer, device_id_type=mesh_ids)
+    first_block = pltpu.make_async_copy(
+        fourier_ref.at[pl.ds(0, ROWS)], block.at[0], block_sem.at[0]
+    )
+    first_block.start()
     pl.semaphore_wait(barrier, len(peers) + len(sides))
 
     def table_copy(chunk, mask):
@@ -79,11 +85,19 @@
             device_id=peers[mask], device_id_type=mesh_ids,
         )
 
-    def later_copy(piece, mask):
-        span = pl.ds(piece * PIECE, PIECE)
+    def last_copy(step, mask):
+        span = pl.ds((chunks - 1) * GROUP + step * PIECE, PIECE)
         return pltpu.make_async_remote_copy(
             src_ref=send_ref.at[mask, span], dst_ref=land_ref.at[mask - 1, span],
-            send_sem=send_sem.at[piece, mask - 1], recv_sem=recv_sem.at[piece, mask - 1],
+            send_sem=send_last.at[step, mask - 1], recv_sem=recv_last.at[step, mask - 1],
+            device_id=peers[mask], device_id_type=mesh_ids,
+        )
+
+    def later_copy(chunk, mask):
+        span = pl.ds(chunk * GROUP, GROUP)
+        return pltpu.make_async_remote_copy(
+            src_ref=send_ref.at[mask, span], dst_ref=land_ref.at[mask - 1, span],
+            send_sem=send_sem.at[chunk, mask - 1], recv_sem=recv_sem.at[chunk, mask - 1],
             device_id=peers[mask], device_id_type=mesh_ids,
         )
 
@@ -93,25 +107,19 @@
         )
 
     def pick(chunk, after):
-        block_copy(0, 0).start()
-
         def one(step, carry):
             side = lax.rem(step, 2)
 
-            @pl.when(step + 1 < blocks)
+            @pl.when((step + 1 < blocks) | (chunk + 1 < chunks))
             def _():
-                block_copy(step + 1, 1 - side).start()
+                block_copy(lax.rem(step + 1, blocks), 1 - side).start()
 
             block_copy(step, side).wait()
 
-            def row(r, inner):
+            for r in range(ROWS):
                 drawn[:, r, :] = jnp.dot(
                     picks_ref[chunk], block[side, r], preferred_element_type=jnp.float32
                 )
-                return inner
-
-            for r in range(ROWS):
-                row(r, 0)
             packed[...] = drawn[...].astype(packed.dtype).reshape(packed.shape)
             copy = pltpu.make_async_copy(
                 packed,
@@ -125,12 +133,9 @@
 
         lax.fori_loop(0, blocks, one, 0)
 
-    def project(piece):
+    def project(piece, arrive):
         span = pl.ds(piece * PIECE, PIECE)
         copies = [pltpu.make_async_copy(send_ref.at[0, span], rows.at[:, me], load_sem.at[0])]
-        for m in order:
-            copies.append(pltpu.make_async_copy(
-                land_ref.at[m - 1, span], rows.at[:, peers[m][0]], load_sem.at[m]))
         for m in range(lev_count):
             source = table_ref.at[span] if m == 0 else tables_ref.at[m - 1, span]
             start = pl.multiple_of((lev if m == 0 else sides[m][1]) * row_count, ROWS)
@@ -138,27 +143,32 @@
                 source, table.at[:, :, pl.ds(start, row_count)], load_sem.at[lat_count + m]))
         for copy in copies:
             copy.start()
+        for m in [*order[lat_count // 2 :], *order[: lat_count // 2]]:
+            arrive(m)
+            copies.append(pltpu.make_async_copy(
+                land_ref.at[m - 1, span], rows.at[:, peers[m][0]], load_sem.at[m]))
+            copies[-1].start()
         for copy in copies:
             copy.wait()
 
         def one(i, carry):
             half = lat_count // 2
+            slot = piece * PIECE + i
             upper = rows[i, :half].astype(jnp.float32).reshape(-1, column_count)
             lower = rows[i, half:].astype(jnp.float32).reshape(-1, column_count)
             even[...] = (upper + lower).astype(even.dtype)
             odd[...] = (upper - lower).astype(odd.dtype)
+            degree = lax.broadcasted_iota(jnp.int32, (half_rows, column_count), 0)
             for parity, part in enumerate((even, odd)):
                 total = lax.dot_general(
                     table[i, parity], part[...], (((0,), (0,)), ((), ())),
                     preferred_element_type=jnp.float32,
                 )
-                made[i, parity] = total.astype(made.dtype)
+                kept = jnp.where(degree < live_ref[slot, parity], total, 0.0)
+                out_ref[slot, parity] = kept.astype(out_ref.dtype)
             return carry
 
         lax.fori_loop(0, PIECE, one, 0)
-        copy = pltpu.make_async_copy(made, out_ref.at[span], store_sem)
-        copy.start()
-        copy.wait()
 
     def start_tables(chunk):
         for m in sides:
@@ -169,22 +179,35 @@
             first_copy(step, m).start()
 
     def send_chunk(chunk):
+        for m in order:
+            later_copy(chunk, m).start()
+
+    def send_last_chunk():
         def one(p, carry):
             for m in order:
-                later_copy(chunk * pieces + p, m).start()
+                last_copy(p, m).start()
             return carry
 
         lax.fori_loop(0, pieces, one, 0)
 
     def project_chunk(chunk):
         def one(p, carry):
-            for m in order:
-                later_copy(chunk * pieces + p, m).wait_recv()
-            project(chunk * pieces + p)
+            project(chunk * pieces + p, nothing)
             return carry
 
         for m in sides:
             table_copy(chunk, m).wait_recv()
+        for m in order:
+            later_copy(chunk, m).wait_recv()
+        lax.fori_loop(0, pieces, one, 0)
+
+    def project_last():
+        def one(p, carry):
+            project((chunks - 1) * pieces + p, lambda m: last_copy(p, m).wait_recv())
+            return carry
+
+        for m in sides:
+            table_copy(chunks - 1, m).wait_recv()
         lax.fori_loop(0, pieces, one, 0)
 
     def first_chunk():
@@ -194,7 +217,7 @@
             return carry
 
         def one(p, carry):
-            project(p)
+            project(p, nothing)
             return carry
 
         for m in sides:
@@ -202,20 +225,26 @@
         lax.fori_loop(0, blocks, landed, 0)
         lax.fori_loop(0, pieces, one, 0)
 
-    def nothing(step):
-        del step
-
-    pick_start = 1
+    def nothing(unused):
+        del unused
+
     pick(0, send_rows)
     start_tables(0)
-    pick(pick_start, nothing)
+    pick(1, nothing)
     start_tables(1)
     send_chunk(1)
 
     def stage(chunk, carry):
         pick(chunk, nothing)
         start_tables(chunk)
-        send_chunk(chunk)
+
+        @pl.when(chunk < chunks - 1)
+        def _():
+            send_chunk(chunk)
+
+        @pl.when(chunk == chunks - 1)
+        def _():
+            send_last_chunk()
 
         @pl.when(chunk == 2)
         def _():
@@ -229,16 +258,21 @@
 
     lax.fori_loop(2, chunks, stage, 0)
     project_chunk(chunks - 2)
-    project_chunk(chunks - 1)
+    project_last()
 
     def drain_first(step, carry):
         for m in order:
             first_copy(step, m).wait_send()
         return carry
 
-    def drain_later(piece, carry):
-        for m in order:
-            later_copy(piece, m).wait_send()
+    def drain_later(chunk, carry):
+        for m in order:
+            later_copy(chunk, m).wait_send()
+        return carry
+
+    def drain_last(step, carry):
+        for m in order:
+            last_copy(step, m).wait_send()
         return carry
 
     def drain_tables(chunk, carry):
@@ -247,7 +281,8 @@
         return carry
 
     lax.fori_loop(0, blocks, drain_first, 0)
-    lax.fori_loop(pieces, chunks * pieces, drain_later, 0)
+    lax.fori_loop(1, chunks - 1, drain_later, 0)
+    lax.fori_loop(0, pieces, drain_last, 0)
     lax.fori_loop(0, chunks, drain_tables, 0)
 
 
@@ -256,7 +291,7 @@
     row_count, wave_count, column_count = fourier.shape
     half_rows = legendre.shape[3]
     slot_count = wave_count // lat_count
-    chunks, blocks, pieces = slot_count // GROUP, row_count // ROWS, slot_count // PIECE
+    chunks, blocks = slot_count // GROUP, row_count // ROWS
     me = lax.axis_index("lat")
     placed = ranks(owner, slot_count)
     shape = (chunks, lat_count, GROUP)
@@ -269,14 +304,19 @@
     own = me * slot_count + jnp.arange(slot_count, dtype=jnp.int32)
     wave_ids = jnp.arange(wave_count, dtype=jnp.int32)
     waves = jnp.sum(jnp.where(placed[None, :] == own[:, None], wave_ids[None, :], 0), axis=1)
+    parity = jnp.arange(2, dtype=jnp.int32)
+    live = (wave_count - waves[:, None] - parity[None, :] + 1) // 2
     dtype = jnp.bfloat16
     anywhere = pl.BlockSpec(memory_space=pl.ANY)
     made, *_ = pl.pallas_call(
         exchange,
-        in_specs=[anywhere, pl.BlockSpec(memory_space=pltpu.VMEM), anywhere],
-        out_specs=[anywhere] * 4,
+        in_specs=[
+            pl.BlockSpec(memory_space=pltpu.SMEM), anywhere,
+            pl.BlockSpec(memory_space=pltpu.VMEM), anywhere,
+        ],
+        out_specs=[pl.BlockSpec(memory_space=pltpu.VMEM), *[anywhere] * 3],
         out_shape=[
-            jax.ShapeDtypeStruct((slot_count, 2, half_rows, column_count), dtype),
+            pltpu.VMEM((slot_count, 2, half_rows, column_count), dtype),
             jax.ShapeDtypeStruct((lat_count, slot_count, row_count, column_count), dtype),
             jax.ShapeDtypeStruct((lat_count - 1, slot_count, row_count, column_count), dtype),
             jax.ShapeDtypeStruct((lev_count - 1, *legendre.shape), dtype),
@@ -287,28 +327,25 @@
             pltpu.VMEM((lat_count, GROUP, ROWS, column_count), dtype),
             pltpu.VMEM((PIECE, lat_count, row_count, column_count), dtype),
             pltpu.VMEM((PIECE, 2, lev_count * row_count, half_rows), dtype),
-            pltpu.VMEM((PIECE, 2, half_rows, column_count), dtype),
             pltpu.VMEM((lat_count // 2 * row_count, column_count), dtype),
             pltpu.VMEM((lat_count // 2 * row_count, column_count), dtype),
             pltpu.SemaphoreType.DMA((2,)),
             pltpu.SemaphoreType.DMA,
             pltpu.SemaphoreType.DMA((blocks, lat_count - 1)),
             pltpu.SemaphoreType.DMA((blocks, lat_count - 1)),
-            pltpu.SemaphoreType.DMA((pieces, lat_count - 1)),
-            pltpu.SemaphoreType.DMA((pieces, lat_count - 1)),
+            pltpu.SemaphoreType.DMA((chunks, lat_count - 1)),
+            pltpu.SemaphoreType.DMA((chunks, lat_count - 1)),
+            pltpu.SemaphoreType.DMA((GROUP // PIECE, lat_count - 1)),
+            pltpu.SemaphoreType.DMA((GROUP // PIECE, lat_count - 1)),
             pltpu.SemaphoreType.DMA((chunks, lev_count - 1)),
             pltpu.SemaphoreType.DMA((chunks, lev_count - 1)),
             pltpu.SemaphoreType.DMA((lat_count + lev_count,)),
-            pltpu.SemaphoreType.DMA,
         ],
         compiler_params=pltpu.CompilerParams(
-            collective_id=0, has_side_effects=True, vmem_limit_bytes=48 * 1024 * 1024
+            collective_id=0, has_side_effects=True, vmem_limit_bytes=32 * 1024 * 1024
         ),
-    )(fourier, picks, legendre)
-    parity = jnp.arange(2, dtype=jnp.int32)
-    live = (wave_count - waves[:, None] - parity[None, :] + 1) // 2
-    degree = lax.broadcasted_iota(jnp.int32, made.shape, 2)
-    return jnp.where(degree < live[:, :, None, None], made, jnp.zeros_like(made))
+    )(live, fourier, picks, legendre)
+    return made
 
 
 def slot_places(owner, slot_count):
@@ -416,7 +453,8 @@
         slot_count = wave_count // lat_count
         fits = (
             direct_fits(mesh)
-            and row_count % ROWS == 0
+            and row_count % (2 * ROWS) == 0
+            and slot_count * legendre.shape[3] * fourier.shape[2] <= MADE_ELEMENTS
             and slot_count % GROUP == 0
             and slot_count // GROUP >= 4
             and row_count * lat_count // 2 == legendre.shape[2] * lev_count

time: 1180 us -> 1160 us (0.983)
  other arithmetic: 27.4 us -> 3.83 us
    select_n x1 -> x0, other arithmetic: 25.1 us -> none  [direct_body(): jnp.where(degree < live[:, :, None, None], made, jnp.zeros_like(made))]
where the time goes in v2:
time: 1160 us
  Pallas kernels  1150 us (99%)
    pallas_call x1, Pallas kernels, direct_body(): pl.pallas_call(exchange, in_specs=[pl.BlockSpec(memory_space=pltpu.SMEM),...  1150 us

profile of v2, /device:TPU:0, one launch (start us, length us, event | category | flops | bytes accessed | tf_op | source)
XLA Modules:
  0.0 1158.8 jit_solution(2794857862896858564)
XLA Ops:
  0.0 0.1 iota.45
  0.1 0.1 mul.33
  0.2 1.1 convert_reduce_fusion
  1.2 0.7 multiply_add_fusion
  1.9 0.2 select_reduce_fusion
  2.1 0.1 iota.50
  2.2 0.1 add_add_fusion
  2.3 0.7 add_select_fusion.live_ref
  3.0 1.1 compare_convert_fusion.picks_ref
  4.1 1145.5 %shard_map.37 = (bf16[80,2,320,256]{3,2,1,0:T(8,128)(2,1)S(1)}, bf16[8,80,160,256]{3,2,1,0:T(8,128)(2,1)}, bf16[7,80,160,256]{3,2,1,0:T(8,128)(2,1)}, bf16[3,80,2,160,320]{4,3,2,1,0:T(8,128)(2,1)}) custom-call(s32[80,2]{1,0:T(8,128)} %add_select_fusion.live_ref, bf16[160,640,256]{2,1,0:T(8,128)(2,1)} %fourier_ref.1, ...), custom_call_target="tpu_custom_call" | custom-call | tf_op jit(solution)/shard_map/pallas_call | solution.py:311
  1149.6 9.3 copy.5
  (5 shorter events, 0.0 us)
